TPU v7x, 32 devices: a whole 2x2x4 slice. The times are simulated.
32 devices in a mesh: expert: 4 (over z), neuron: 8 (over y, x, core).
Axes of the slice: x: 2, y: 2, z: 4, core: 2. Of those that a mesh axis runs over, the one named last changes fastest.
Arguments:
- tokens: bfloat16 [256, 4096], P('neuron'), may hold values from -6 to 6
- route_logits: float32 [256, 2], replicated, may hold values from -6 to 6
- expert_ids: int32 [256, 2], replicated, may hold values from 0 to 3, all different within a row; in each aligned block of 256 rows (0 to 255, 256 to 511, ...) at most 128 rows name the same one
- block_live: int32 [4, 224], P('expert', 'neuron'), may hold values 0 or 1
- w_gate: bfloat16 [4, 4096, 14336], P('expert', None, 'neuron'), may hold values from -0.09375 to 0.09375
- w_up: bfloat16 [4, 4096, 14336], P('expert', None, 'neuron'), may hold values from -0.09375 to 0.09375
- w_down: bfloat16 [4, 14336, 4096], P('expert', 'neuron'), may hold values from -0.046875 to 0.046875
Outputs:
- mixed: bfloat16 [256, 4096], P('neuron')
Inputs may be any that keep to these rules, and one draw needn't show every extreme that they name: `expert_ids`: each token names two different experts; no expert is named by more than 128 tokens, a bound that some block reaches; every expert is named.
All inputs are finite; a program needn't handle non-finite values. No bound on the sum of `block_live` on one device may be relied on, other than what follows from the above.
Results may differ from a plain program's by a relative error of at most 0.0049.
Values may be sent and summed in bfloat16 or wider, within the bound.
A program may use at most 128 MiB of HBM per device.

v0:
```python
import jax
import jax.numpy as jnp
from jax import lax
from jax.sharding import PartitionSpec as P

BLK = 64


def routing(expert_ids, route_logits, expert, capacity):
    chosen = (expert_ids == expert).astype(jnp.int32)
    flat_hits = chosen.reshape(-1)
    before = (jnp.cumsum(flat_hits) - flat_hits).reshape(chosen.shape)
    slot_pair = jnp.where(chosen > 0, before, capacity)
    leading = jax.nn.sigmoid(route_logits[:, 0] - route_logits[:, 1])
    mix_gates = jnp.stack([leading, 1.0 - leading], axis=1)
    weight = jnp.sum(mix_gates * chosen.astype(jnp.float32), axis=1)
    slot_tok = jnp.min(slot_pair, axis=1)
    slot_index = lax.broadcasted_iota(jnp.int32, (capacity, expert_ids.shape[0]), 0)
    dispatch = (
        (slot_pair[None, :, 0] == slot_index) | (slot_pair[None, :, 1] == slot_index)
    ).astype(jnp.bfloat16)
    return (dispatch, slot_tok, weight)


def per_device(tokens, route_logits, expert_ids, block_live, w_gate, w_up, w_down):
    total_tokens = expert_ids.shape[0]
    capacity = total_tokens // 2
    expert = lax.axis_index("expert")
    dispatch, slot_tok, weight = routing(expert_ids, route_logits, expert, capacity)
    gathered = jnp.dot(
        dispatch,
        lax.all_gather(tokens, "neuron", axis=0, tiled=True),
        preferred_element_type=jnp.float32,
    ).astype(jnp.bfloat16)
    gate_val = jnp.dot(gathered, w_gate[0], preferred_element_type=jnp.float32)
    up_val = jnp.dot(gathered, w_up[0], preferred_element_type=jnp.float32)
    live = jnp.repeat(block_live[0].astype(jnp.float32), BLK)
    hidden = (jax.nn.silu(gate_val) * up_val * live[None, :]).astype(jnp.bfloat16)
    partial_value = jnp.dot(hidden, w_down[0], preferred_element_type=jnp.float32)
    picked = jnp.take(partial_value, jnp.minimum(slot_tok, capacity - 1), axis=0)
    weighted = weight[:, None] * picked
    own_part = lax.psum_scatter(weighted, "neuron", scatter_dimension=0, tiled=True)
    mixed = lax.psum(own_part, "expert")
    return mixed.astype(jnp.bfloat16)


def solution(mesh):
    placed = (
        P("neuron", None),
        P(),
        P(),
        P("expert", "neuron"),
        P("expert", None, "neuron"),
        P("expert", None, "neuron"),
        P("expert", "neuron", None),
    )
    return jax.shard_map(
        per_device, mesh=mesh, in_specs=placed, out_specs=P("neuron", None), check_vma=False
    )
```

profile of v0, /device:TPU:0, one launch (start us, length us, event | category | flops | bytes accessed | tf_op | source)
XLA Modules:
  0.0 162.3 jit_solution(13914430239259568634)
XLA Ops:
  6.5 0.0 all-gather.2.cloned.1.call-start
  6.5 0.7 all-gather.2.cloned.1.call-update
  7.3 0.0 reduce-scatter.2.cloned.1.call-start
  7.3 0.8 broadcast_subtract_fusion
  8.1 0.7 fusion.23
  8.8 0.1 copy.21
  8.9 0.1 reshape.51
  9.1 0.3 reduce-window.9
  9.4 0.1 slice.21
  9.5 0.1 reshape.52
  9.6 0.7 convert_bitcast_fusion
  10.3 0.1 broadcast_in_dim.20
  10.3 0.1 mul.32
  10.4 0.1 slice_reduce_fusion
  10.6 0.1 broadcast.55
  10.6 0.1 reshape.54
  10.7 0.1 copy.22
  10.9 28.9 %all-gather.2.cloned.1.call-done = bf16[256,4096]{1,0:T(8,128)(2,1)} async-done(((bf16[32,4096]{1,0:T(8,128)(2,1)}), bf16[256,4096]{1,0:T(8,128)(2,1)}) %all-gather.2.cloned.1.call-update) | async-done | bytes 2097168 | tf_op jit(solution)/shard_map/all_gather | solution.py:32
  39.8 2.0 %convolution_convert_fusion = bf16[128,4096]{1,0:T(8,128)(2,1)S(1)} fusion(bf16[256,4096]{1,0:T(8,128)(2,1)} %all-gather.2.cloned.1.call-done, s32[256]{0:T(256)S(1)} %bitcast.27, s32[256]{0:T(256)S(1)} %bitcast.26), kind=kOutput, calls=%fused_computation.7 | convolution fusion | flops 269058048 | bytes 3147776 | tf_op jit(solution)/shard_map/dot_general | solution.py:30
  41.8 8.2 %fusion.4 = f32[128,1792]{1,0:T(8,128)} fusion(bf16[128,4096]{1,0:T(8,128)(2,1)S(1)} %convolution_convert_fusion, bf16[1,4096,1792]{2,1,0:T(8,128)(2,1)} %param.11), kind=kOutput, calls=%fused_computation.5 | convolution fusion | flops 1879048192 | bytes 16646144 | tf_op jit(solution)/shard_map/dot_general | solution.py:35
  50.0 14.1 %fusion = f32[128,4096]{1,0:T(8,128)S(1)} fusion(bf16[1,1792,4096]{2,1,0:T(8,128)(2,1)} %param.13, bf16[128,4096]{1,0:T(8,128)(2,1)S(1)} %convolution_convert_fusion, bf16[1,4096,1792]{2,1,0:T(8,128)(2,1)} %param.12, f32[128,1792]{1,0:T(8,128)} %fusion.4, f32[1792]{0:T(1024)S(1)} %mul.32), kind=kOutput, calls=%fused_computation.1 | convolution fusion | flops 3759702016 | bytes 33430528 | tf_op jit(solution)/shard_map/dot_general | solution.py:39
  64.1 3.8 %gather_fusion = f32[256,4096]{1,0:T(8,128)} fusion(f32[128,4096]{1,0:T(8,128)S(1)} %fusion, s32[1024]{0:T(1024)S(1)} %pad_clamp_fusion), kind=kCustom, calls=%fused_computation | custom fusion | bytes 8389632 | tf_op jit(solution)/shard_map/jit(_take)/gather | solution.py:40
  67.9 4.9 %select_multiply_fusion = f32[256,4096]{1,0:T(8,128)} fusion(f32[256,4096]{1,0:T(8,128)} %gather_fusion, f32[256]{0:T(256)S(1)} %get-tuple-element.5, pred[256]{0:T(512)(128)(4,1)S(1)} %compare_and_fusion), kind=kLoop, calls=%fused_computation.8 | loop fusion | flops 2097152 | bytes 8389888 | tf_op jit(solution)/shard_map/mul | solution.py:41
  72.8 0.0 reduce-scatter.2.cloned.1.call-update
  72.8 51.3 %reduce-scatter.2.cloned.1.call-done = f32[32,4096]{1,0:T(8,128)} async-done(((f32[256,4096]{1,0:T(8,128)}), f32[32,4096]{1,0:T(8,128)}) %reduce-scatter.2.cloned.1.call-update) | async-done | bytes 524304 | tf_op jit(solution)/shard_map/reduce_scatter | solution.py:42
  124.1 31.4 %all-reduce.1 = bf16[32,4096]{1,0:T(8,128)(2,1)} all-reduce(f32[32,4096]{1,0:T(8,128)} %reduce-scatter.2.cloned.1.call-done), channel_id=1, replica_groups=mesh['expert'=4,'neuron'=8] {'expert'}, use_global_device_ids=true, to_apply=%region_5.6 | all-reduce | flops 131072 | bytes 786432 | tf_op jit(solution)/shard_map/psum | solution.py:43
  (7 shorter events, 0.1 us)
Async XLA Ops:
  6.5 33.2 %all-gather.2.cloned.1.call-start = ((), (), s32[]{:S(2)}) async-start(), calls=%async_computation.1 | async-start | bytes 2359296 | tf_op jit(solution)/shard_map/all_gather | solution.py:32
  7.3 116.8 %reduce-scatter.2.cloned.1.call-start = ((), (), s32[]{:S(2)}) async-start(), calls=%async_computation.2 | async-start | bytes 4718592 | tf_op jit(solution)/shard_map/reduce_scatter | solution.py:42
Sparse Core Ops, SparseCore 0:
  9.2 30.5 all-gather.1
  72.9 51.1 reduce-scatter.1
where the time goes:
time: 163 us; the launch traced here: 162 us
  waiting for transfers between devices  80.9 us (50%)
  blocking collectives  31.4 us (19%)
  matrix products  24.3 us (15%)
  between operations  13.5 us (8%)
  other arithmetic  7.42 us (5%)
  local copies, waits for them, and re-layouts  4.83 us (3%)
    reduce_scatter x1, waiting for transfers between devices, per_device(): lax.psum_scatter(weighted, 'neuron', scatter_dimension=0, tiled=True)  51.3 us
    psum x1, blocking collectives, per_device(): mixed = lax.psum(own_part, 'expert')  31.4 us
    all_gather x1, waiting for transfers between devices, per_device(): lax.all_gather(tokens, 'neuron', axis=0, tiled=True)  28.9 us
    dot_general x1, matrix products, per_device(): jnp.dot(hidden, w_down[0], preferred_element_type=jnp.float32)  14.1 us
    dot_general x1, matrix products, per_device(): gate_val = jnp.dot(gathered, w_gate[0], preferred_element_type=jnp.float32)  8.18 us
    mul x1, other arithmetic, per_device(): weighted = weight[:, None] * picked  4.89 us
    gather x1, local copies, waits for them, and re-layouts, per_device(): jnp.take(partial_value, jnp.minimum(slot_tok, capacity - 1), axis=0)  3.82 us
  transfers between devices with their start and end apart: 2, of which 2 were waited for; matrix products, arithmetic and copies ran while one was open for 2% of the time, Pallas kernels for 0%

commit v1 on v0

--- a/solution.py
+++ b/solution.py
@@ -40,7 +40,9 @@
     picked = jnp.take(partial_value, jnp.minimum(slot_tok, capacity - 1), axis=0)
     weighted = weight[:, None] * picked
     own_part = lax.psum_scatter(weighted, "neuron", scatter_dimension=0, tiled=True)
-    mixed = lax.psum(own_part, "expert")
+    mixed = own_part
+    for hop in (1, 2):
+        mixed = mixed + lax.ppermute(mixed, "expert", [(dev, dev ^ hop) for dev in range(4)])
     return mixed.astype(jnp.bfloat16)
 
 

time: 163 us -> 172 us (1.055)
  waiting for transfers between devices: 80.9 us -> 115 us
  blocking collectives: 31.4 us -> 0 us
  starting transfers between devices: 0.04 us -> 3.99 us
  other arithmetic: 7.42 us -> 9.29 us
    ppermute x0 -> x2, waiting for transfers between devices: none -> 34.6 us  [per_device(): lax.ppermute(mixed, 'expert', [(dev, dev ^ hop) for dev in range(4)])]
    psum x1 -> x0, blocking collectives: 31.4 us -> none  [per_device(): mixed = lax.psum(own_part, 'expert')]
    ppermute x0 -> x2, starting transfers between devices: none -> 3.95 us  [per_device(): lax.ppermute(mixed, 'expert', [(dev, dev ^ hop) for dev in range(4)])]
  transfers between devices with their start and end apart: 2 -> 4, of which waited for: 2 -> 4; matrix products, arithmetic and copies ran while one was open for 2% -> 2% of each run, Pallas kernels for 0% -> 0%
where the time goes in v1:
time: 172 us; the launch traced here: 171 us
  waiting for transfers between devices  115 us (67%)
  matrix products  24.3 us (14%)
  between operations  13.5 us (8%)
  other arithmetic  9.29 us (5%)
  local copies, waits for them, and re-layouts  4.83 us (3%)
  starting transfers between devices  3.99 us (2%)
    reduce_scatter x1, waiting for transfers between devices, per_device(): lax.psum_scatter(weighted, 'neuron', scatter_dimension=0, tiled=True)  51.3 us
    ppermute x2, waiting for transfers between devices, per_device(): lax.ppermute(mixed, 'expert', [(dev, dev ^ hop) for dev in range(4)])  34.6 us
    all_gather x1, waiting for transfers between devices, per_device(): lax.all_gather(tokens, 'neuron', axis=0, tiled=True)  28.9 us
    dot_general x1, matrix products, per_device(): jnp.dot(hidden, w_down[0], preferred_element_type=jnp.float32)  14.1 us
    dot_general x1, matrix products, per_device(): gate_val = jnp.dot(gathered, w_gate[0], preferred_element_type=jnp.float32)  8.18 us
    mul x1, other arithmetic, per_device(): weighted = weight[:, None] * picked  4.89 us
    ppermute x2, starting transfers between devices, per_device(): lax.ppermute(mixed, 'expert', [(dev, dev ^ hop) for dev in range(4)])  3.95 us
    gather x1, local copies, waits for them, and re-layouts, per_device(): jnp.take(partial_value, jnp.minimum(slot_tok, capacity - 1), axis=0)  3.82 us
  transfers between devices with their start and end apart: 4, of which 4 were waited for; matrix products, arithmetic and copies ran while one was open for 2% of the time, Pallas kernels for 0%

profile of v1, /device:TPU:0, one launch (start us, length us, event | category | flops | bytes accessed | tf_op | source)
XLA Modules:
  0.0 171.4 jit_solution(8700124053685484241)
XLA Ops:
  6.5 0.0 all-gather.2.cloned.1.call-start
  6.5 0.7 all-gather.2.cloned.1.call-update
  7.3 0.0 reduce-scatter.2.cloned.1.call-start
  7.3 0.8 broadcast_subtract_fusion
  8.1 0.7 fusion.23
  8.8 0.1 copy.21
  8.9 0.1 reshape.51
  9.1 0.3 reduce-window.9
  9.4 0.1 slice.21
  9.5 0.1 reshape.52
  9.6 0.7 convert_bitcast_fusion
  10.3 0.1 broadcast_in_dim.20
  10.3 0.1 mul.32
  10.4 0.1 slice_reduce_fusion
  10.6 0.1 broadcast.55
  10.6 0.1 reshape.54
  10.7 0.1 copy.22
  10.9 28.9 %all-gather.2.cloned.1.call-done = bf16[256,4096]{1,0:T(8,128)(2,1)} async-done(((bf16[32,4096]{1,0:T(8,128)(2,1)}), bf16[256,4096]{1,0:T(8,128)(2,1)}) %all-gather.2.cloned.1.call-update) | async-done | bytes 2097168 | tf_op jit(solution)/shard_map/all_gather | solution.py:32
  39.8 2.0 %convolution_convert_fusion = bf16[128,4096]{1,0:T(8,128)(2,1)S(1)} fusion(bf16[256,4096]{1,0:T(8,128)(2,1)} %all-gather.2.cloned.1.call-done, s32[256]{0:T(256)S(1)} %bitcast.27, s32[256]{0:T(256)S(1)} %bitcast.26), kind=kOutput, calls=%fused_computation.7 | convolution fusion | flops 269058048 | bytes 3147776 | tf_op jit(solution)/shard_map/dot_general | solution.py:30
  41.8 8.2 %fusion.4 = f32[128,1792]{1,0:T(8,128)} fusion(bf16[128,4096]{1,0:T(8,128)(2,1)S(1)} %convolution_convert_fusion, bf16[1,4096,1792]{2,1,0:T(8,128)(2,1)} %param.11), kind=kOutput, calls=%fused_computation.5 | convolution fusion | flops 1879048192 | bytes 16646144 | tf_op jit(solution)/shard_map/dot_general | solution.py:35
  50.0 14.1 %fusion = f32[128,4096]{1,0:T(8,128)S(1)} fusion(bf16[1,1792,4096]{2,1,0:T(8,128)(2,1)} %param.13, bf16[128,4096]{1,0:T(8,128)(2,1)S(1)} %convolution_convert_fusion, bf16[1,4096,1792]{2,1,0:T(8,128)(2,1)} %param.12, f32[128,1792]{1,0:T(8,128)} %fusion.4, f32[1792]{0:T(1024)S(1)} %mul.32), kind=kOutput, calls=%fused_computation.1 | convolution fusion | flops 3759702016 | bytes 33430528 | tf_op jit(solution)/shard_map/dot_general | solution.py:39
  64.1 3.8 %gather_fusion = f32[256,4096]{1,0:T(8,128)} fusion(f32[128,4096]{1,0:T(8,128)S(1)} %fusion, s32[1024]{0:T(1024)S(1)} %pad_clamp_fusion), kind=kCustom, calls=%fused_computation | custom fusion | bytes 8389632 | tf_op jit(solution)/shard_map/jit(_take)/gather | solution.py:40
  67.9 4.9 %select_multiply_fusion = f32[256,4096]{1,0:T(8,128)} fusion(f32[256,4096]{1,0:T(8,128)} %gather_fusion, f32[256]{0:T(256)S(1)} %get-tuple-element.5, pred[256]{0:T(512)(128)(4,1)S(1)} %compare_and_fusion), kind=kLoop, calls=%fused_computation.8 | loop fusion | flops 2097152 | bytes 8389888 | tf_op jit(solution)/shard_map/mul | solution.py:41
  72.8 0.0 reduce-scatter.2.cloned.1.call-update
  72.8 51.3 %reduce-scatter.2.cloned.1.call-done = f32[32,4096]{1,0:T(8,128)} async-done(((f32[256,4096]{1,0:T(8,128)}), f32[32,4096]{1,0:T(8,128)}) %reduce-scatter.2.cloned.1.call-update) | async-done | bytes 524304 | tf_op jit(solution)/shard_map/reduce_scatter | solution.py:42
  124.1 1.5 collective-permute-start
  125.6 12.2 %collective-permute-done = f32[32,4096]{1,0:T(8,128)S(1)} collective-permute-done((f32[32,4096]{1,0:T(8,128)}, f32[32,4096]{1,0:T(8,128)S(1)}, u32[]{:S(2)}, u32[]{:S(2)}) %collective-permute-start) | collective-permute-done | bytes 524320 | tf_op jit(solution)/shard_map/ppermute | solution.py:45
  137.8 1.1 add.44
  138.9 2.5 %collective-permute-start.1 = (f32[32,4096]{1,0:T(8,128)S(1)}, f32[32,4096]{1,0:T(8,128)S(1)}, u32[]{:S(2)}, u32[]{:S(2)}) collective-permute-start(f32[32,4096]{1,0:T(8,128)S(1)} %add.44), channel_id=1, source_target_pairs={{0,16},{8,24},{16,0},{24,8},{1,17},{9,25},{17,1},{25,9},{2,18},{10... | collective-permute-start | bytes 1572872 | tf_op jit(solution)/shard_map/ppermute | solution.py:45
  141.4 22.4 %collective-permute-done.1 = f32[32,4096]{1,0:T(8,128)S(1)} collective-permute-done((f32[32,4096]{1,0:T(8,128)S(1)}, f32[32,4096]{1,0:T(8,128)S(1)}, u32[]{:S(2)}, u32[]{:S(2)}) %collective-permute-start.1) | collective-permute-done | bytes 524320 | tf_op jit(solution)/shard_map/ppermute | solution.py:45
  163.8 0.8 add_convert_fusion
  (7 shorter events, 0.1 us)
Async XLA Ops:
  6.5 33.2 %all-gather.2.cloned.1.call-start = ((), (), s32[]{:S(2)}) async-start(), calls=%async_computation.1 | async-start | bytes 2359296 | tf_op jit(solution)/shard_map/all_gather | solution.py:32
  7.3 116.8 %reduce-scatter.2.cloned.1.call-start = ((), (), s32[]{:S(2)}) async-start(), calls=%async_computation.2 | async-start | bytes 4718592 | tf_op jit(solution)/shard_map/reduce_scatter | solution.py:42
  124.1 13.7 %collective-permute-start = (f32[32,4096]{1,0:T(8,128)}, f32[32,4096]{1,0:T(8,128)S(1)}, u32[]{:S(2)}, u32[]{:S(2)}) collective-permute-start(f32[32,4096]{1,0:T(8,128)} %reduce-scatter.2.cloned.1.call-done), channel_id=1, source_target_pairs={{0,8},{8,0},{16,24},{24,16},{1,9},{9,1},{17,25},{25,17},{2,10},{10... | collective-permute-start | bytes 1572872 | tf_op jit(solution)/shard_map/ppermute | solution.py:45
  138.9 24.8 %collective-permute-start.1 = (f32[32,4096]{1,0:T(8,128)S(1)}, f32[32,4096]{1,0:T(8,128)S(1)}, u32[]{:S(2)}, u32[]{:S(2)}) collective-permute-start(f32[32,4096]{1,0:T(8,128)S(1)} %add.44), channel_id=1, source_target_pairs={{0,16},{8,24},{16,0},{24,8},{1,17},{9,25},{17,1},{25,9},{2,18},{10... | collective-permute-start | bytes 1572872 | tf_op jit(solution)/shard_map/ppermute | solution.py:45
Sparse Core Ops, SparseCore 0:
  9.2 30.5 all-gather.1
  72.9 51.1 reduce-scatter.1
